TPU v7x, 32 devices: a whole 2x2x4 slice. The times are simulated.
32 devices in a mesh: trial: 4 (over z), south: 2 (over core), east: 2 (over x), down: 2 (over y).
Axes of the slice: x: 2, y: 2, z: 4, core: 2. Of those that a mesh axis runs over, the one named last changes fastest.
Arguments:
- tracer: float32 [32, 32, 256, 128], P(('trial', 'south'), 'east', 'down'), parts along dimension 0, may hold values from 0.5 to 2
- mobility: float32 [32, 32, 256, 128], P(('trial', 'south'), 'east', 'down'), parts along dimension 0, may hold values from 0.03 to 0.15
- source: float32 [32, 32, 256, 128], P(('trial', 'south'), 'east', 'down'), parts along dimension 0, may hold values from -0.2 to 0.2
Outputs:
- standardized: float32 [32, 32, 256, 128], P(('trial', 'south'), 'east', 'down'), parts along dimension 0
- tracer_end: float32 [32, 32, 256, 128], P(('trial', 'south'), 'east', 'down'), parts along dimension 0
There are 4 independent parts, one for each index of `trial`. A program takes and returns all parts, laid end to end along the dimension named above; each array names one. Nothing has to cross between parts.
All inputs are finite; a program needn't handle non-finite values.
Results may differ from a plain program's by a relative error of at most 0.00002.
Values sent between devices are 32-bit elements; how exact they have to be, the bound alone decides.
A program may use at most 128 MiB of HBM per device.

v0:
```python
import jax
import jax.numpy as jnp
from jax import lax
from jax.sharding import PartitionSpec as P

STEPS = 3


def with_halo(block, sides, width):
    for axis, dim in sides:
        count = lax.axis_size(axis)
        forward = [(i, i + 1) for i in range(count - 1)]
        forward.append((count - 1, 0))
        backward = [(target, source) for source, target in forward]
        low = lax.ppermute(
            lax.slice_in_dim(block, block.shape[dim] - width, None, axis=dim), axis, forward
        )
        high = lax.ppermute(lax.slice_in_dim(block, 0, width, axis=dim), axis, backward)
        block = jnp.concatenate([low, block, high], axis=dim)
    return block


def strip_edges(values, dims):
    for dim in dims:
        values = lax.slice_in_dim(values, 1, values.shape[dim] - 1, axis=dim)
    return values


def neighbour(values, dim, start, dims):
    others = [other for other in dims if other != dim]
    values = strip_edges(values, others)
    return lax.slice_in_dim(values, start, start + values.shape[dim] - 2, axis=dim)


def one_step(padded, mobility, source):
    middle = strip_edges(padded, (0, 1, 2))
    lower = [neighbour(padded, dim, 0, (0, 1, 2)) for dim in (0, 1, 2)]
    upper = [neighbour(padded, dim, 2, (0, 1, 2)) for dim in (0, 1, 2)]
    spread = lower[0] + upper[0] + lower[1] + upper[1] + lower[2] + upper[2] - 6.0 * middle
    return middle + mobility * spread + source


def body(tracer, mobility, source):
    for step in range(STEPS):
        padded = with_halo(tracer, (("south", 0), ("east", 1), ("down", 2)), 1)
        tracer = one_step(padded, mobility, source)
    count = tracer.shape[2] * lax.axis_size("down")
    line_mean = lax.psum(jnp.sum(tracer, axis=2, keepdims=True), "down") / count
    centred = tracer - line_mean
    line_variance = lax.psum(jnp.sum(centred * centred, axis=2, keepdims=True), "down") / count
    standardized = centred * lax.rsqrt(line_variance + 0.0001)
    return (standardized, tracer)


def solution(mesh):
    in_specs = (
        P(("trial", "south"), "east", "down", None),
        P(("trial", "south"), "east", "down", None),
        P(("trial", "south"), "east", "down", None),
    )
    out_specs = (
        P(("trial", "south"), "east", "down", None),
        P(("trial", "south"), "east", "down", None),
    )
    return jax.shard_map(body, mesh=mesh, in_specs=in_specs, out_specs=out_specs, check_vma=False)
```

profile of v0, /device:TPU:0, one launch (start us, length us, event | category | flops | bytes accessed | tf_op | source)
XLA Modules:
  0.0 147.4 jit_solution(11715911265367690488)
XLA Ops:
  0.6 1.8 %fusion.32 = (f32[1,16,128,128]{3,2,1,0:T(8,128)S(1)}, f32[1,16,128,128]{3,2,1,0:T(8,128)S(1)}) fusion(f32[4,16,128,128]{3,2,1,0:T(8,128)} %param.3), kind=kLoop, calls=%fused_computation.103 | loop fusion | bytes 4194304 | tf_op jit(solution)/shard_map/slice | solution.py:18
  2.5 0.6 collective-permute-start
  3.0 0.1 collective-permute-start.1
  3.1 2.2 %collective-permute-done = f32[1,16,128,128]{3,2,1,0:T(8,128)S(1)} collective-permute-done((f32[1,16,128,128]{3,2,1,0:T(8,128)S(1)}, f32[1,16,128,128]{3,2,1,0:T(8,128)S(1)}, u32[]{:S(2)}, u32[]{:S(2)}) %collective-permute-start) | collective-permute-done | bytes 1048608 | tf_op jit(solution)/shard_map/ppermute | solution.py:15
  5.3 0.1 constant_dynamic-update-slice_fusion.2
  5.4 0.5 constant_dynamic-update-slice_fusion.1
  5.9 0.9 collective-permute-done.1
  6.8 0.1 constant_dynamic-update-slice_fusion
  7.0 2.9 %collective-permute-start.2 = (f32[6,1,128,128]{3,2,1,0:T(8,128)S(1)}, f32[6,1,128,128]{3,2,1,0:T(8,128)S(1)}, u32[]{:S(2)}, u32[]{:S(2)}) collective-permute-start(f32[6,1,128,128]{3,2,1,0:T(8,128)S(1)} %get-tuple-element.14), channel_id=1, source_target_pairs={{0,2},{2,0},{1,3},{3,1},{4,6},{6,4},{5,7},{7,5},{8,10},{10,8},{9,1... | collective-permute-start | bytes 1179656 | tf_op jit(solution)/shard_map/ppermute | solution.py:15
  9.9 0.1 collective-permute-start.3
  10.0 9.9 %collective-permute-done.2 = f32[6,1,128,128]{3,2,1,0:T(8,128)S(1)} collective-permute-done((f32[6,1,128,128]{3,2,1,0:T(8,128)S(1)}, f32[6,1,128,128]{3,2,1,0:T(8,128)S(1)}, u32[]{:S(2)}, u32[]{:S(2)}) %collective-permute-start.2) | collective-permute-done | bytes 393248 | tf_op jit(solution)/shard_map/ppermute | solution.py:15
  19.9 7.9 %collective-permute-done.3 = f32[6,1,128,128]{3,2,1,0:T(8,128)S(1)} collective-permute-done((f32[6,1,128,128]{3,2,1,0:T(8,128)S(1)}, f32[6,1,128,128]{3,2,1,0:T(8,128)S(1)}, u32[]{:S(2)}, u32[]{:S(2)}) %collective-permute-start.3) | collective-permute-done | bytes 393248 | tf_op jit(solution)/shard_map/ppermute | solution.py:18
  27.8 0.1 pad_maximum_fusion.64
  27.9 1.8 %collective-permute-start.4 = (f32[6,18,1,128]{3,2,1,0:T(1,128)S(1)}, f32[6,18,1,128]{3,2,1,0:T(1,128)S(1)}, u32[]{:S(2)}, u32[]{:S(2)}) collective-permute-start(f32[6,18,1,128]{3,2,1,0:T(1,128)S(1)} %get-tuple-element.8), channel_id=1, source_target_pairs={{0,1},{1,0},{2,3},{3,2},{4,5},{5,4},{6,7},{7,6},{8,9},{9,8},{10,11... | collective-permute-start | bytes 165896 | tf_op jit(solution)/shard_map/ppermute | solution.py:15
  29.7 0.3 collective-permute-start.5
  29.9 2.5 %collective-permute-done.4 = f32[6,18,1,128]{3,2,1,0:T(1,128)S(1)} collective-permute-done((f32[6,18,1,128]{3,2,1,0:T(1,128)S(1)}, f32[6,18,1,128]{3,2,1,0:T(1,128)S(1)}, u32[]{:S(2)}, u32[]{:S(2)}) %collective-permute-start.4) | collective-permute-done | bytes 55328 | tf_op jit(solution)/shard_map/ppermute | solution.py:15
  32.5 1.4 collective-permute-done.5
  33.8 13.8 %fusion.22 = f32[4,16,128,128]{3,2,1,0:T(8,128)S(1)} fusion(f32[4,16,128,128]{3,2,1,0:T(8,128)S(1)} %copy-done, f32[4,16,128,128]{3,2,1,0:T(8,128)} %param.3, f32[4,16,128,128]{3,2,1,0:T(8,128)} %param.4, f32[6,18,1,128]{3,2,1,0:T(1,128)S(1)} %collective-permute-done.5, f32[6,1,128,128]{3,2,1,0:T(8,128)S(1)} %collective-permute-done.3, ...), kind=kLoop, calls=%fused_computation.59 | loop fusion | flops 20971520 | bytes 26062848 | tf_op jit(solution)/shard_map/add | solution.py:40
  47.6 0.1 fusion.31
  47.8 0.5 collective-permute-start.7
  48.3 2.1 %collective-permute-done.6 = f32[1,16,128,128]{3,2,1,0:T(8,128)S(1)} collective-permute-done((f32[1,16,128,128]{3,2,1,0:T(8,128)S(1)}, f32[1,16,128,128]{3,2,1,0:T(8,128)S(1)}, u32[]{:S(2)}, u32[]{:S(2)}) %collective-permute-start.6) | collective-permute-done | bytes 1048608 | tf_op jit(solution)/shard_map/ppermute | solution.py:15
  50.5 1.5 %collective-permute-done.7 = f32[1,16,128,128]{3,2,1,0:T(8,128)S(1)} collective-permute-done((f32[1,16,128,128]{3,2,1,0:T(8,128)S(1)}, f32[1,16,128,128]{3,2,1,0:T(8,128)S(1)}, u32[]{:S(2)}, u32[]{:S(2)}) %collective-permute-start.7) | collective-permute-done | bytes 1048608 | tf_op jit(solution)/shard_map/ppermute | solution.py:18
  52.1 1.6 %collective-permute-start.8 = (f32[6,1,128,128]{3,2,1,0:T(8,128)S(1)}, f32[6,1,128,128]{3,2,1,0:T(8,128)S(1)}, u32[]{:S(2)}, u32[]{:S(2)}) collective-permute-start(f32[6,1,128,128]{3,2,1,0:T(8,128)S(1)} %get-tuple-element.12), channel_id=1, source_target_pairs={{0,2},{2,0},{1,3},{3,1},{4,6},{6,4},{5,7},{7,5},{8,10},{10,8},{9,1... | collective-permute-start | bytes 1179656 | tf_op jit(solution)/shard_map/ppermute | solution.py:15
  53.6 0.5 collective-permute-start.9
  54.2 10.0 %collective-permute-done.8 = f32[6,1,128,128]{3,2,1,0:T(8,128)S(1)} collective-permute-done((f32[6,1,128,128]{3,2,1,0:T(8,128)S(1)}, f32[6,1,128,128]{3,2,1,0:T(8,128)S(1)}, u32[]{:S(2)}, u32[]{:S(2)}) %collective-permute-start.8) | collective-permute-done | bytes 393248 | tf_op jit(solution)/shard_map/ppermute | solution.py:15
  64.1 7.6 %collective-permute-done.9 = f32[6,1,128,128]{3,2,1,0:T(8,128)S(1)} collective-permute-done((f32[6,1,128,128]{3,2,1,0:T(8,128)S(1)}, f32[6,1,128,128]{3,2,1,0:T(8,128)S(1)}, u32[]{:S(2)}, u32[]{:S(2)}) %collective-permute-start.9) | collective-permute-done | bytes 393248 | tf_op jit(solution)/shard_map/ppermute | solution.py:18
  71.8 0.7 collective-permute-start.10
  72.5 1.4 collective-permute-start.11
  73.9 2.1 %collective-permute-done.10 = f32[6,18,1,128]{3,2,1,0:T(1,128)S(1)} collective-permute-done((f32[6,18,1,128]{3,2,1,0:T(1,128)S(1)}, f32[6,18,1,128]{3,2,1,0:T(1,128)S(1)}, u32[]{:S(2)}, u32[]{:S(2)}) %collective-permute-start.10) | collective-permute-done | bytes 55328 | tf_op jit(solution)/shard_map/ppermute | solution.py:15
  76.0 0.6 collective-permute-done.11
  76.6 7.6 %fusion.13 = f32[4,16,128,128]{3,2,1,0:T(8,128)S(1)} fusion(f32[4,16,128,128]{3,2,1,0:T(8,128)S(1)} %copy-done, f32[4,16,128,128]{3,2,1,0:T(8,128)S(1)} %fusion.22, f32[4,16,128,128]{3,2,1,0:T(8,128)S(1)} %copy-done.1, f32[6,18,1,128]{3,2,1,0:T(1,128)S(1)} %collective-permute-done.11, f32[6,1,128,128]{3,2,1,0:T(8,128)S(1)} %collective-permute-done.9, ...), kind=kLoop, calls=%fused_computation.32 | loop fusion | flops 29360128 | bytes 19771392 | tf_op jit(solution)/shard_map/add | solution.py:40
  84.2 0.2 fusion.30
  84.5 0.5 collective-permute-start.13
  85.0 2.1 %collective-permute-done.12 = f32[1,16,128,128]{3,2,1,0:T(8,128)S(1)} collective-permute-done((f32[1,16,128,128]{3,2,1,0:T(8,128)S(1)}, f32[1,16,128,128]{3,2,1,0:T(8,128)S(1)}, u32[]{:S(2)}, u32[]{:S(2)}) %collective-permute-start.12) | collective-permute-done | bytes 1048608 | tf_op jit(solution)/shard_map/ppermute | solution.py:15
  87.2 1.5 %collective-permute-done.13 = f32[1,16,128,128]{3,2,1,0:T(8,128)S(1)} collective-permute-done((f32[1,16,128,128]{3,2,1,0:T(8,128)S(1)}, f32[1,16,128,128]{3,2,1,0:T(8,128)S(1)}, u32[]{:S(2)}, u32[]{:S(2)}) %collective-permute-start.13) | collective-permute-done | bytes 1048608 | tf_op jit(solution)/shard_map/ppermute | solution.py:18
  88.7 1.6 %collective-permute-start.14 = (f32[6,1,128,128]{3,2,1,0:T(8,128)S(1)}, f32[6,1,128,128]{3,2,1,0:T(8,128)S(1)}, u32[]{:S(2)}, u32[]{:S(2)}) collective-permute-start(f32[6,1,128,128]{3,2,1,0:T(8,128)S(1)} %get-tuple-element.10), channel_id=1, source_target_pairs={{0,2},{2,0},{1,3},{3,1},{4,6},{6,4},{5,7},{7,5},{8,10},{10,8},{9,1... | collective-permute-start | bytes 1179656 | tf_op jit(solution)/shard_map/ppermute | solution.py:15
  90.3 0.5 collective-permute-start.15
  90.8 10.0 %collective-permute-done.14 = f32[6,1,128,128]{3,2,1,0:T(8,128)S(1)} collective-permute-done((f32[6,1,128,128]{3,2,1,0:T(8,128)S(1)}, f32[6,1,128,128]{3,2,1,0:T(8,128)S(1)}, u32[]{:S(2)}, u32[]{:S(2)}) %collective-permute-start.14) | collective-permute-done | bytes 393248 | tf_op jit(solution)/shard_map/ppermute | solution.py:15
  100.8 7.6 %collective-permute-done.15 = f32[6,1,128,128]{3,2,1,0:T(8,128)S(1)} collective-permute-done((f32[6,1,128,128]{3,2,1,0:T(8,128)S(1)}, f32[6,1,128,128]{3,2,1,0:T(8,128)S(1)}, u32[]{:S(2)}, u32[]{:S(2)}) %collective-permute-start.15) | collective-permute-done | bytes 393248 | tf_op jit(solution)/shard_map/ppermute | solution.py:18
  108.4 1.5 %collective-permute-start.16 = (f32[6,18,1,128]{3,2,1,0:T(1,128)S(1)}, f32[6,18,1,128]{3,2,1,0:T(1,128)S(1)}, u32[]{:S(2)}, u32[]{:S(2)}) collective-permute-start(f32[6,18,1,128]{3,2,1,0:T(1,128)S(1)} %get-tuple-element.4), channel_id=1, source_target_pairs={{0,1},{1,0},{2,3},{3,2},{4,5},{5,4},{6,7},{7,6},{8,9},{9,8},{10,11... | collective-permute-start | bytes 165896 | tf_op jit(solution)/shard_map/ppermute | solution.py:15
  109.9 0.6 collective-permute-start.17
  110.5 2.2 %collective-permute-done.16 = f32[6,18,1,128]{3,2,1,0:T(1,128)S(1)} collective-permute-done((f32[6,18,1,128]{3,2,1,0:T(1,128)S(1)}, f32[6,18,1,128]{3,2,1,0:T(1,128)S(1)}, u32[]{:S(2)}, u32[]{:S(2)}) %collective-permute-start.16) | collective-permute-done | bytes 55328 | tf_op jit(solution)/shard_map/ppermute | solution.py:15
  112.7 1.4 collective-permute-done.17
  114.1 9.3 %fusion.27 = (f32[4,16,128]{2,1,0:T(8,128)S(1)}, f32[4,16,128,128]{3,2,1,0:T(8,128)}) fusion(f32[4,16,128,128]{3,2,1,0:T(8,128)S(1)} %copy-done, f32[4,16,128,128]{3,2,1,0:T(8,128)S(1)} %fusion.13, f32[4,16,128,128]{3,2,1,0:T(8,128)S(1)} %copy-done.1, f32[6,18,1,128]{3,2,1,0:T(1,128)S(1)} %collective-permute-done.17, ...), kind=kLoop, calls=%fused_computation.99 | loop fusion | flops 30400512 | bytes 19804160 | tf_op jit(solution)/shard_map/reduce_sum | solution.py:48
  123.4 7.4 %psum.14 = f32[4,16,1,128]{3,1,0,2:T(8,128)S(1)} all-reduce(f32[4,16,1,128]{3,1,0,2:T(8,128)S(1)} %bitcast.6), channel_id=1, replica_groups=mesh['trial'=4,'south'=2,'east'=2,'down'=2] {'down'}, use_global_device_ids=true, to_apply=%region_1.0 | all-reduce | flops 8192 | bytes 65536 | tf_op jit(solution)/shard_map/psum | solution.py:48
  130.8 3.0 %multiply_reduce_fusion = f32[4,16,128]{2,1,0:T(8,128)S(1)} fusion(f32[4,16,128,128]{3,2,1,0:T(8,128)} %get-tuple-element.3, f32[4,16,128]{2,1,0:T(8,128)S(1)} %multiply_bitcast_fusion), kind=kLoop, calls=%fused_computation.73 | loop fusion | flops 3137536 | bytes 4259840 | tf_op jit(solution)/shard_map/reduce_sum | solution.py:50
  133.8 8.3 %psum.15 = f32[4,16,1,128]{3,1,0,2:T(8,128)S(1)} all-reduce(f32[4,16,1,128]{3,1,0,2:T(8,128)S(1)} %bitcast.7), channel_id=1, replica_groups=mesh['trial'=4,'south'=2,'east'=2,'down'=2] {'down'}, use_global_device_ids=true, to_apply=%region_3.0 | all-reduce | flops 8192 | bytes 65536 | tf_op jit(solution)/shard_map/psum | solution.py:50
  142.1 5.2 %subtract_multiply_fusion = f32[4,16,128,128]{3,2,1,0:T(8,128)} fusion(f32[4,16,128,128]{3,2,1,0:T(8,128)} %get-tuple-element.3, f32[4,16,128]{2,1,0:T(8,128)S(1)} %rsqrt_bitcast_fusion, f32[4,16,128]{2,1,0:T(8,128)S(1)} %multiply_bitcast_fusion), kind=kLoop, calls=%fused_computation.74 | loop fusion | flops 2097152 | bytes 8454144 | tf_op jit(solution)/shard_map/mul | solution.py:51
  (17 shorter events, 0.5 us)
Async XLA Ops:
  0.6 4.8 %copy-start.3 = (f32[4,16,128,128]{3,2,1,0:T(8,128)S(1)}, f32[4,16,128,128]{3,2,1,0:T(8,128)}, u32[]{:S(2)}) copy-start(f32[4,16,128,128]{3,2,1,0:T(8,128)} %param.3) | copy-start | bytes 12582916
  2.5 2.8 %collective-permute-start = (f32[1,16,128,128]{3,2,1,0:T(8,128)S(1)}, f32[1,16,128,128]{3,2,1,0:T(8,128)S(1)}, u32[]{:S(2)}, u32[]{:S(2)}) collective-permute-start(f32[1,16,128,128]{3,2,1,0:T(8,128)S(1)} %get-tuple-element.21), channel_id=1, source_target_pairs={{0,4},{4,0},{1,5},{5,1},{2,6},{6,2},{3,7},{7,3},{8,12},{12,8},{9,1... | collective-permute-start | bytes 3145736 | tf_op jit(solution)/shard_map/ppermute | solution.py:15
  3.0 3.8 %collective-permute-start.1 = (f32[1,16,128,128]{3,2,1,0:T(8,128)S(1)}, f32[1,16,128,128]{3,2,1,0:T(8,128)S(1)}, u32[]{:S(2)}, u32[]{:S(2)}) collective-permute-start(f32[1,16,128,128]{3,2,1,0:T(8,128)S(1)} %get-tuple-element.20), channel_id=1, source_target_pairs={{4,0},{0,4},{5,1},{1,5},{6,2},{2,6},{7,3},{3,7},{12,8},{8,12},{13,... | collective-permute-start | bytes 3145736 | tf_op jit(solution)/shard_map/ppermute | solution.py:18
  6.9 25.5 %copy-start.2 = (f32[6,16,128,128]{3,2,1,0:T(8,128)}, f32[6,16,128,128]{3,2,1,0:T(8,128)S(1)}, u32[]{:S(2)}) copy-start(f32[6,16,128,128]{3,2,1,0:T(8,128)S(1)} %constant_dynamic-update-slice_fusion) | copy-start | bytes 18874372
  6.9 26.9 %copy-start = (f32[4,16,128,128]{3,2,1,0:T(8,128)S(1)}, f32[4,16,128,128]{3,2,1,0:T(8,128)}, u32[]{:S(2)}) copy-start(f32[4,16,128,128]{3,2,1,0:T(8,128)} %param.5) | copy-start | bytes 12582916
  7.0 12.9 %collective-permute-start.2 = (f32[6,1,128,128]{3,2,1,0:T(8,128)S(1)}, f32[6,1,128,128]{3,2,1,0:T(8,128)S(1)}, u32[]{:S(2)}, u32[]{:S(2)}) collective-permute-start(f32[6,1,128,128]{3,2,1,0:T(8,128)S(1)} %get-tuple-element.14), channel_id=1, source_target_pairs={{0,2},{2,0},{1,3},{3,1},{4,6},{6,4},{5,7},{7,5},{8,10},{10,8},{9,1... | collective-permute-start | bytes 1179656 | tf_op jit(solution)/shard_map/ppermute | solution.py:15
  9.9 17.8 %collective-permute-start.3 = (f32[6,1,128,128]{3,2,1,0:T(8,128)S(1)}, f32[6,1,128,128]{3,2,1,0:T(8,128)S(1)}, u32[]{:S(2)}, u32[]{:S(2)}) collective-permute-start(f32[6,1,128,128]{3,2,1,0:T(8,128)S(1)} %get-tuple-element.15), channel_id=1, source_target_pairs={{2,0},{0,2},{3,1},{1,3},{6,4},{4,6},{7,5},{5,7},{10,8},{8,10},{11,... | collective-permute-start | bytes 1179656 | tf_op jit(solution)/shard_map/ppermute | solution.py:18
  27.9 4.6 %collective-permute-start.4 = (f32[6,18,1,128]{3,2,1,0:T(1,128)S(1)}, f32[6,18,1,128]{3,2,1,0:T(1,128)S(1)}, u32[]{:S(2)}, u32[]{:S(2)}) collective-permute-start(f32[6,18,1,128]{3,2,1,0:T(1,128)S(1)} %get-tuple-element.8), channel_id=1, source_target_pairs={{0,1},{1,0},{2,3},{3,2},{4,5},{5,4},{6,7},{7,6},{8,9},{9,8},{10,11... | collective-permute-start | bytes 165896 | tf_op jit(solution)/shard_map/ppermute | solution.py:15
  29.7 4.2 %collective-permute-start.5 = (f32[6,18,1,128]{3,2,1,0:T(1,128)S(1)}, f32[6,18,1,128]{3,2,1,0:T(1,128)S(1)}, u32[]{:S(2)}, u32[]{:S(2)}) collective-permute-start(f32[6,18,1,128]{3,2,1,0:T(1,128)S(1)} %get-tuple-element.9), channel_id=1, source_target_pairs={{1,0},{0,1},{3,2},{2,3},{5,4},{4,5},{7,6},{6,7},{9,8},{8,9},{11,10... | collective-permute-start | bytes 165896 | tf_op jit(solution)/shard_map/ppermute | solution.py:18
  47.8 2.7 %collective-permute-start.6 = (f32[1,16,128,128]{3,2,1,0:T(8,128)S(1)}, f32[1,16,128,128]{3,2,1,0:T(8,128)S(1)}, u32[]{:S(2)}, u32[]{:S(2)}) collective-permute-start(f32[1,16,128,128]{3,2,1,0:T(8,128)S(1)} %get-tuple-element.18), channel_id=1, source_target_pairs={{0,4},{4,0},{1,5},{5,1},{2,6},{6,2},{3,7},{7,3},{8,12},{12,8},{9,1... | collective-permute-start | bytes 3145736 | tf_op jit(solution)/shard_map/ppermute | solution.py:15
  47.8 4.1 %collective-permute-start.7 = (f32[1,16,128,128]{3,2,1,0:T(8,128)S(1)}, f32[1,16,128,128]{3,2,1,0:T(8,128)S(1)}, u32[]{:S(2)}, u32[]{:S(2)}) collective-permute-start(f32[1,16,128,128]{3,2,1,0:T(8,128)S(1)} %get-tuple-element.19), channel_id=1, source_target_pairs={{4,0},{0,4},{5,1},{1,5},{6,2},{2,6},{7,3},{3,7},{12,8},{8,12},{13,... | collective-permute-start | bytes 3145736 | tf_op jit(solution)/shard_map/ppermute | solution.py:18
  52.1 24.6 %copy-start.1 = (f32[4,16,128,128]{3,2,1,0:T(8,128)S(1)}, f32[4,16,128,128]{3,2,1,0:T(8,128)}, u32[]{:S(2)}) copy-start(f32[4,16,128,128]{3,2,1,0:T(8,128)} %param.4) | copy-start | bytes 12582916
  52.1 12.1 %collective-permute-start.8 = (f32[6,1,128,128]{3,2,1,0:T(8,128)S(1)}, f32[6,1,128,128]{3,2,1,0:T(8,128)S(1)}, u32[]{:S(2)}, u32[]{:S(2)}) collective-permute-start(f32[6,1,128,128]{3,2,1,0:T(8,128)S(1)} %get-tuple-element.12), channel_id=1, source_target_pairs={{0,2},{2,0},{1,3},{3,1},{4,6},{6,4},{5,7},{7,5},{8,10},{10,8},{9,1... | collective-permute-start | bytes 1179656 | tf_op jit(solution)/shard_map/ppermute | solution.py:15
  53.6 18.1 %collective-permute-start.9 = (f32[6,1,128,128]{3,2,1,0:T(8,128)S(1)}, f32[6,1,128,128]{3,2,1,0:T(8,128)S(1)}, u32[]{:S(2)}, u32[]{:S(2)}) collective-permute-start(f32[6,1,128,128]{3,2,1,0:T(8,128)S(1)} %get-tuple-element.13), channel_id=1, source_target_pairs={{2,0},{0,2},{3,1},{1,3},{6,4},{4,6},{7,5},{5,7},{10,8},{8,10},{11,... | collective-permute-start | bytes 1179656 | tf_op jit(solution)/shard_map/ppermute | solution.py:18
  71.8 4.2 %collective-permute-start.10 = (f32[6,18,1,128]{3,2,1,0:T(1,128)S(1)}, f32[6,18,1,128]{3,2,1,0:T(1,128)S(1)}, u32[]{:S(2)}, u32[]{:S(2)}) collective-permute-start(f32[6,18,1,128]{3,2,1,0:T(1,128)S(1)} %get-tuple-element.6), channel_id=1, source_target_pairs={{0,1},{1,0},{2,3},{3,2},{4,5},{5,4},{6,7},{7,6},{8,9},{9,8},{10,11... | collective-permute-start | bytes 165896 | tf_op jit(solution)/shard_map/ppermute | solution.py:15
  72.5 4.2 %collective-permute-start.11 = (f32[6,18,1,128]{3,2,1,0:T(1,128)S(1)}, f32[6,18,1,128]{3,2,1,0:T(1,128)S(1)}, u32[]{:S(2)}, u32[]{:S(2)}) collective-permute-start(f32[6,18,1,128]{3,2,1,0:T(1,128)S(1)} %get-tuple-element.7), channel_id=1, source_target_pairs={{1,0},{0,1},{3,2},{2,3},{5,4},{4,5},{7,6},{6,7},{9,8},{8,9},{11,10... | collective-permute-start | bytes 165896 | tf_op jit(solution)/shard_map/ppermute | solution.py:18
  84.4 2.7 %collective-permute-start.12 = (f32[1,16,128,128]{3,2,1,0:T(8,128)S(1)}, f32[1,16,128,128]{3,2,1,0:T(8,128)S(1)}, u32[]{:S(2)}, u32[]{:S(2)}) collective-permute-start(f32[1,16,128,128]{3,2,1,0:T(8,128)S(1)} %get-tuple-element.16), channel_id=1, source_target_pairs={{0,4},{4,0},{1,5},{5,1},{2,6},{6,2},{3,7},{7,3},{8,12},{12,8},{9,1... | collective-permute-start | bytes 3145736 | tf_op jit(solution)/shard_map/ppermute | solution.py:15
  84.5 4.1 %collective-permute-start.13 = (f32[1,16,128,128]{3,2,1,0:T(8,128)S(1)}, f32[1,16,128,128]{3,2,1,0:T(8,128)S(1)}, u32[]{:S(2)}, u32[]{:S(2)}) collective-permute-start(f32[1,16,128,128]{3,2,1,0:T(8,128)S(1)} %get-tuple-element.17), channel_id=1, source_target_pairs={{4,0},{0,4},{5,1},{1,5},{6,2},{2,6},{7,3},{3,7},{12,8},{8,12},{13,... | collective-permute-start | bytes 3145736 | tf_op jit(solution)/shard_map/ppermute | solution.py:18
  88.7 12.1 %collective-permute-start.14 = (f32[6,1,128,128]{3,2,1,0:T(8,128)S(1)}, f32[6,1,128,128]{3,2,1,0:T(8,128)S(1)}, u32[]{:S(2)}, u32[]{:S(2)}) collective-permute-start(f32[6,1,128,128]{3,2,1,0:T(8,128)S(1)} %get-tuple-element.10), channel_id=1, source_target_pairs={{0,2},{2,0},{1,3},{3,1},{4,6},{6,4},{5,7},{7,5},{8,10},{10,8},{9,1... | collective-permute-start | bytes 1179656 | tf_op jit(solution)/shard_map/ppermute | solution.py:15
  90.3 18.1 %collective-permute-start.15 = (f32[6,1,128,128]{3,2,1,0:T(8,128)S(1)}, f32[6,1,128,128]{3,2,1,0:T(8,128)S(1)}, u32[]{:S(2)}, u32[]{:S(2)}) collective-permute-start(f32[6,1,128,128]{3,2,1,0:T(8,128)S(1)} %get-tuple-element.11), channel_id=1, source_target_pairs={{2,0},{0,2},{3,1},{1,3},{6,4},{4,6},{7,5},{5,7},{10,8},{8,10},{11,... | collective-permute-start | bytes 1179656 | tf_op jit(solution)/shard_map/ppermute | solution.py:18
  108.4 4.3 %collective-permute-start.16 = (f32[6,18,1,128]{3,2,1,0:T(1,128)S(1)}, f32[6,18,1,128]{3,2,1,0:T(1,128)S(1)}, u32[]{:S(2)}, u32[]{:S(2)}) collective-permute-start(f32[6,18,1,128]{3,2,1,0:T(1,128)S(1)} %get-tuple-element.4), channel_id=1, source_target_pairs={{0,1},{1,0},{2,3},{3,2},{4,5},{5,4},{6,7},{7,6},{8,9},{9,8},{10,11... | collective-permute-start | bytes 165896 | tf_op jit(solution)/shard_map/ppermute | solution.py:15
  109.9 4.2 %collective-permute-start.17 = (f32[6,18,1,128]{3,2,1,0:T(1,128)S(1)}, f32[6,18,1,128]{3,2,1,0:T(1,128)S(1)}, u32[]{:S(2)}, u32[]{:S(2)}) collective-permute-start(f32[6,18,1,128]{3,2,1,0:T(1,128)S(1)} %get-tuple-element.5), channel_id=1, source_target_pairs={{1,0},{0,1},{3,2},{2,3},{5,4},{4,5},{7,6},{6,7},{9,8},{8,9},{11,10... | collective-permute-start | bytes 165896 | tf_op jit(solution)/shard_map/ppermute | solution.py:18
where the time goes:
time: 148 us; the launch traced here: 147 us
  waiting for transfers between devices  73.5 us (50%)
  other arithmetic  39.2 us (26%)
  blocking collectives  15.7 us (11%)
  starting transfers between devices  15.2 us (10%)
  local copies, waits for them, and re-layouts  2.94 us (2%)
    ppermute x9, waiting for transfers between devices, with_halo(): lax.ppermute(lax.slice_in_dim(block, block.shape[dim] - width, None, axis...  43.1 us
    ppermute x9, waiting for transfers between devices, with_halo(): lax.ppermute(lax.slice_in_dim(block, 0, width, axis=dim), axis, backward)  30.3 us
    add x2, other arithmetic, one_step(): return middle + mobility * spread + source  21.3 us
    ppermute x9, starting transfers between devices, with_halo(): lax.ppermute(lax.slice_in_dim(block, block.shape[dim] - width, None, axis...  10.7 us
    reduce_sum x1, other arithmetic, body(): line_mean = lax.psum(jnp.sum(tracer, axis=2, keepdims=True), 'down') / count  9.27 us
    psum x1, blocking collectives, body(): lax.psum(jnp.sum(centred * centred, axis=2, keepdims=True), 'down') / count  8.28 us
    psum x1, blocking collectives, body(): line_mean = lax.psum(jnp.sum(tracer, axis=2, keepdims=True), 'down') / count  7.43 us
    mul x2, other arithmetic, body(): standardized = centred * lax.rsqrt(line_variance + 0.0001)  5.24 us
  transfers between devices with their start and end apart: 18, of which 18 were waited for; matrix products, arithmetic and copies ran while one was open for 0% of the time, Pallas kernels for 0%

commit v1 on v0

v1 whole, which is shorter than its diff:
```python
import functools

import jax
import jax.numpy as jnp
from jax import lax
from jax.experimental import pallas as pl
from jax.experimental.pallas import tpu as pltpu
from jax.sharding import PartitionSpec as P

MESH = pl.DeviceIdType.MESH
PAD = 8
ROWS = 32
EPS = 0.0001


def kernel(
    counts, tracer, mobility, source, standardized, end,
    t0, t1, t2, mob, src, stats,
    load_sem, x_send, x_recv, y_send, y_recv, z_send, z_recv, s_send, s_recv,
):
    ny, nx, nz, _ = mob.shape
    n_down = counts["down"]
    me = {axis: lax.axis_index(axis) for axis in counts}

    def peer(axis, offset):
        count = counts[axis]
        return {axis: lax.rem(me[axis] + (offset % count), count)}

    fields = (t0, t1, t2)
    line = pl.ds(PAD, nz)
    low, high, middle = (pl.ds(1, 1), pl.ds(nx, 1), pl.ds(2, nx - 2))
    groups = (middle, low, high)

    def load(sem, array, into):
        return pltpu.make_async_copy(array, into, load_sem.at[sem])

    def load_field(sem, columns):
        inside = pl.ds(columns.start - 1, columns.size)
        return load(sem, tracer.at[:, inside], t0.at[pl.ds(1, ny), columns, line])

    loads = [load_field(i, c) for i, c in enumerate((low, high, middle))]
    loads += [load(3, mobility, mob), load(4, source, src)]
    for copy in loads:
        copy.start()

    def send(field, from_, to, sems, at, device):
        return pltpu.make_async_remote_copy(
            src_ref=field.at[from_],
            dst_ref=field.at[to],
            send_sem=sems[0].at[at],
            recv_sem=sems[1].at[at],
            device_id=device,
            device_id_type=MESH,
        )

    inner_y = pl.ds(1, ny)

    def face(step, side):
        from_, to, offset = ((1, nx + 1, -1), (nx, 0, 1))[side]
        return send(
            fields[step],
            (inner_y, pl.ds(from_, 1), line),
            (inner_y, pl.ds(to, 1), line),
            (x_send, x_recv), (step, side), peer("east", offset),
        )

    def borders(step, group):
        columns = groups[group]
        field = fields[step]
        copies = []
        for side, (from_, to, offset) in enumerate(((1, ny + 1, -1), (ny, 0, 1))):
            copies.append(send(
                field, (pl.ds(from_, 1), columns, line), (pl.ds(to, 1), columns, line),
                (y_send, y_recv), (step, side, group), peer("south", offset),
            ))
        for side, (from_, to, offset) in enumerate(
            ((PAD, PAD + nz, -1), (PAD + nz - 1, PAD - 1, 1))
        ):
            copies.append(send(
                field, (inner_y, columns, pl.ds(from_, 1)), (inner_y, columns, pl.ds(to, 1)),
                (z_send, z_recv), (step, side, group), peer("down", offset),
            ))
        return copies

    def moments(group):
        columns = groups[group]
        inside = pl.ds(columns.start - 1, columns.size)
        return [
            pltpu.make_async_remote_copy(
                src_ref=stats.at[0, inside],
                dst_ref=stats.at[j, inside],
                send_sem=s_send.at[j - 1, group],
                recv_sem=s_recv.at[j - 1, group],
                device_id=peer("down", j),
                device_id_type=MESH,
            )
            for j in range(1, n_down)
        ]

    started = []

    def start(copies):
        for copy in copies:
            copy.start()
            started.append(copy)

    barrier = pltpu.get_barrier_semaphore()
    greeted = [peer("south", -1), peer("south", 1), peer("east", -1), peer("east", 1)]
    greeted += [peer("down", j) for j in range(1, n_down)]
    for device in greeted:
        pl.semaphore_signal(barrier, inc=1, device_id=device, device_id_type=MESH)
    pl.semaphore_wait(barrier, len(greeted))

    faces = [[face(step, side) for side in (0, 1)] for step in range(3)]
    edges = [[borders(step, group) for group in range(3)] for step in range(3)]
    spread_moments = [moments(group) for group in range(3)]

    def column(step, x):
        field = fields[step]
        for z in range(0, nz, ROWS):
            at = pl.ds(PAD + z, ROWS)
            before, after = pl.ds(PAD + z - 1, ROWS), pl.ds(PAD + z + 1, ROWS)
            rows = pl.ds(z, ROWS)
            lines = [field[y, x, at] for y in range(ny + 2)]
            for y in range(1, ny + 1):
                mid = lines[y]
                total = lines[y - 1] + lines[y + 1]
                total += field[y, x - 1, at] + field[y, x + 1, at]
                total += field[y, x, before] + field[y, x, after]
                total -= 6.0 * mid
                new = mid + mob[y - 1, x - 1, rows] * total + src[y - 1, x - 1, rows]
                if step < 2:
                    fields[step + 1][y, x, at] = new
                else:
                    end[y - 1, x - 1, rows] = new

    def measure(x):
        for y in range(ny):
            values = end[y, x - 1]
            mean = jnp.sum(values, axis=0, keepdims=True) * (1.0 / nz)
            off = values - mean
            stats[0, x - 1, pl.ds(y, 1)] = mean
            stats[0, x - 1, pl.ds(ny + y, 1)] = jnp.sum(off * off, axis=0, keepdims=True)

    def finish(x):
        for y in range(ny):
            means = [stats[j, x - 1, pl.ds(y, 1)] for j in range(n_down)]
            mean = sum(means[1:], means[0]) * (1.0 / n_down)
            squares = stats[0, x - 1, pl.ds(ny + y, 1)]
            for j in range(1, n_down):
                squares += stats[j, x - 1, pl.ds(ny + y, 1)]
            for value in means:
                squares += nz * ((value - mean) * (value - mean))
            scale = lax.rsqrt(squares * (1.0 / (nz * n_down)) + EPS)
            for z in range(0, nz, ROWS):
                rows = pl.ds(z, ROWS)
                standardized[y, x - 1, rows] = (end[y, x - 1, rows] - mean) * scale

    def over_middle(work):
        @pl.loop(2, nx)
        def _(x):
            work(x)

    def received(copies):
        for copy in copies:
            copy.wait_recv()

    loads[0].wait()
    start([faces[0][0]])
    loads[1].wait()
    start([faces[0][1]])
    loads[2].wait()
    for group in range(3):
        start(edges[0][group])
    loads[3].wait()
    loads[4].wait()
    for group in range(3):
        received(edges[0][group])
    over_middle(functools.partial(column, 0))
    start(edges[1][0])

    received([faces[0][0]])
    column(0, nx)
    start([faces[1][1]])
    start(edges[1][2])

    received([faces[0][1]])
    column(0, 1)
    start([faces[1][0]])
    start(edges[1][1])

    received(edges[1][0])
    over_middle(functools.partial(column, 1))
    start(edges[2][0])

    received([faces[1][1]])
    received(edges[1][1])
    column(1, 1)
    start([faces[2][0]])
    start(edges[2][1])

    received([faces[1][0]])
    received(edges[1][2])
    column(1, nx)
    start([faces[2][1]])
    start(edges[2][2])

    def last(x):
        column(2, x)
        measure(x)

    received(edges[2][0])
    over_middle(last)
    start(spread_moments[0])
    received(spread_moments[0])
    over_middle(finish)

    received([faces[2][0]])
    received(edges[2][2])
    last(nx)
    start(spread_moments[2])
    received(spread_moments[2])
    finish(nx)

    received([faces[2][1]])
    received(edges[2][1])
    last(1)
    start(spread_moments[1])
    received(spread_moments[1])
    finish(1)

    for copy in started:
        copy.wait_send()


def solution(mesh):
    counts = {axis: mesh.shape[axis] for axis in ("south", "east", "down")}
    spec = P(("trial", "south"), "east", "down", None)

    def body(tracer, mobility, source):
        ny, nx, nz, levels = tracer.shape
        block = jax.ShapeDtypeStruct(tracer.shape, tracer.dtype)
        padded = pltpu.VMEM((ny + 2, nx + 2, nz + 2 * PAD, levels), jnp.float32)
        held = pltpu.VMEM(tracer.shape, jnp.float32)
        n_down = counts["down"]
        dma = pltpu.SemaphoreType.DMA
        return pl.pallas_call(
            functools.partial(kernel, counts),
            out_shape=(block, block),
            in_specs=[pl.BlockSpec(memory_space=pl.ANY)] * 3,
            out_specs=[pl.BlockSpec(memory_space=pltpu.VMEM)] * 2,
            scratch_shapes=[
                padded, padded, padded, held, held,
                pltpu.VMEM((n_down, nx, 2 * ny, levels), jnp.float32),
                dma((5,)),
                dma((3, 2)), dma((3, 2)),
                dma((3, 2, 3)), dma((3, 2, 3)),
                dma((3, 2, 3)), dma((3, 2, 3)),
                dma((n_down - 1, 3)), dma((n_down - 1, 3)),
            ],
            compiler_params=pltpu.CompilerParams(
                collective_id=0, has_side_effects=True, vmem_limit_bytes=60 * 1024 * 1024
            ),
        )(tracer, mobility, source)

    return jax.shard_map(
        body, mesh=mesh, in_specs=(spec,) * 3, out_specs=(spec,) * 2, check_vma=False
    )
```

time: 148 us -> 53.4 us (0.36)
  waiting for transfers between devices: 73.5 us -> 0 us
  Pallas kernels: 0 us -> 45.8 us
  other arithmetic: 39.2 us -> 0 us
  blocking collectives: 15.7 us -> 0 us
  starting transfers between devices: 15.2 us -> 0 us
  local copies, waits for them, and re-layouts: 2.94 us -> 6.87 us
    ppermute x18 -> x0, waiting for transfers between devices: 73.5 us -> none  [the longest x9 43.1 us: with_halo(): lax.ppermute(lax.slice_in_dim(block, block.shape[dim] - width, None, axis...]
    pallas_call x0 -> x1, Pallas kernels: none -> 45.8 us  [body(): pl.pallas_call(functools.partial(kernel, counts), out_shape=(block, block...]
    add x2 -> x0, other arithmetic: 21.3 us -> none  [one_step(): return middle + mobility * spread + source]
    psum x2 -> x0, blocking collectives: 15.7 us -> none  [the longest x1 8.28 us: body(): lax.psum(jnp.sum(centred * centred, axis=2, keepdims=True), 'down') / count]
    ppermute x18 -> x0, starting transfers between devices: 15.2 us -> none  [the longest x9 10.7 us: with_halo(): lax.ppermute(lax.slice_in_dim(block, block.shape[dim] - width, None, axis...]
    reduce_sum x2 -> x0, other arithmetic: 12.3 us -> none  [the longest x1 9.27 us: body(): line_mean = lax.psum(jnp.sum(tracer, axis=2, keepdims=True), 'down') / count]
    unnamed x10 -> x4, local copies, waits for them, and re-layouts: 0.6 us -> 6.87 us
    mul x2 -> x0, other arithmetic: 5.24 us -> none  [body(): standardized = centred * lax.rsqrt(line_variance + 0.0001)]
  transfers between devices with their start and end apart: 18 -> 0, of which waited for: 18 -> 0; matrix products, arithmetic and copies ran while one was open for 0% -> 0% of each run, Pallas kernels for 0% -> 0%
where the time goes in v1:
time: 53.4 us; the launch traced here: 53.3 us
  Pallas kernels  45.8 us (86%)
  local copies, waits for them, and re-layouts  6.87 us (13%)
  between operations  0.65 us (1%)
    pallas_call x1, Pallas kernels, body(): pl.pallas_call(functools.partial(kernel, counts), out_shape=(block, block...  45.8 us
    unnamed x4, local copies, waits for them, and re-layouts  6.87 us

profile of v1, /device:TPU:0, one launch (start us, length us, event | category | flops | bytes accessed | tf_op | source)
XLA Modules:
  0.0 53.3 jit_solution(4909414684572419914)
XLA Ops:
  0.6 45.8 %shard_map.50 = (f32[4,16,128,128]{3,2,1,0:T(8,128)}, f32[4,16,128,128]{3,2,1,0:T(8,128)}) custom-call(f32[4,16,128,128]{3,2,1,0:T(8,128)} %tracer.1, f32[4,16,128,128]{3,2,1,0:T(8,128)} %mobility.1, f32[4,16,128,128]{3,2,1,0:T(8,128)} %source.1), custom_call_target="tpu_custom_call" | custom-call | tf_op jit(solution)/shard_map/pallas_call | solution.py:247
  46.4 0.0 copy-start
  46.4 4.8 %copy.7 = f32[4,16,128,128]{3,2,1,0:T(8,128)} copy(f32[4,16,128,128]{3,2,1,0:T(8,128)} %get-tuple-element.4) | data formatting | bytes 8388608
  51.3 0.0 copy-done
  51.3 2.0 %copy.8 = f32[4,16,128,128]{3,2,1,0:T(8,128)} copy(f32[4,16,128,128]{3,2,1,0:T(8,128)S(1)} %copy-done) | data formatting | bytes 8388608
Async XLA Ops:
  46.4 4.9 %copy-start = (f32[4,16,128,128]{3,2,1,0:T(8,128)S(1)}, f32[4,16,128,128]{3,2,1,0:T(8,128)}, u32[]{:S(2)}) copy-start(f32[4,16,128,128]{3,2,1,0:T(8,128)} %get-tuple-element.5) | copy-start | bytes 12582916

commit v2 on v1

--- a/solution.py
+++ b/solution.py
@@ -233,21 +233,34 @@
         copy.wait_send()
 
 
+def write_out(standardized, end, standardized_out, end_out, sem):
+    pairs = ((standardized, standardized_out), (end, end_out))
+    copies = [
+        pltpu.make_async_copy(held.at[y], out.at[y], sem.at[i, y])
+        for y in range(end.shape[0])
+        for i, (held, out) in enumerate(pairs)
+    ]
+    for copy in copies:
+        copy.start()
+    for copy in copies:
+        copy.wait()
+
+
 def solution(mesh):
     counts = {axis: mesh.shape[axis] for axis in ("south", "east", "down")}
     spec = P(("trial", "south"), "east", "down", None)
 
     def body(tracer, mobility, source):
         ny, nx, nz, levels = tracer.shape
-        block = jax.ShapeDtypeStruct(tracer.shape, tracer.dtype)
+        block = pltpu.VMEM(tracer.shape, tracer.dtype)
         padded = pltpu.VMEM((ny + 2, nx + 2, nz + 2 * PAD, levels), jnp.float32)
         held = pltpu.VMEM(tracer.shape, jnp.float32)
         n_down = counts["down"]
         dma = pltpu.SemaphoreType.DMA
-        return pl.pallas_call(
+        held_outputs = pl.pallas_call(
             functools.partial(kernel, counts),
             out_shape=(block, block),
-            in_specs=[pl.BlockSpec(memory_space=pl.ANY)] * 3,
+            in_specs=[pl.BlockSpec(memory_space=pltpu.HBM)] * 3,
             out_specs=[pl.BlockSpec(memory_space=pltpu.VMEM)] * 2,
             scratch_shapes=[
                 padded, padded, padded, held, held,
@@ -259,9 +272,17 @@
                 dma((n_down - 1, 3)), dma((n_down - 1, 3)),
             ],
             compiler_params=pltpu.CompilerParams(
-                collective_id=0, has_side_effects=True, vmem_limit_bytes=60 * 1024 * 1024
+                collective_id=0, has_side_effects=True, vmem_limit_bytes=54 * 1024 * 1024
             ),
         )(tracer, mobility, source)
+        return pl.pallas_call(
+            write_out,
+            out_shape=(pltpu.HBM(tracer.shape, tracer.dtype),) * 2,
+            in_specs=[pl.BlockSpec(memory_space=pltpu.VMEM)] * 2,
+            out_specs=[pl.BlockSpec(memory_space=pltpu.HBM)] * 2,
+            scratch_shapes=[dma((2, ny))],
+            compiler_params=pltpu.CompilerParams(vmem_limit_bytes=40 * 1024 * 1024),
+        )(*[pltpu.with_memory_space_constraint(held, pltpu.VMEM) for held in held_outputs])
 
     return jax.shard_map(
         body, mesh=mesh, in_specs=(spec,) * 3, out_specs=(spec,) * 2, check_vma=False

time: 53.4 us -> 46.7 us (0.87)
  local copies, waits for them, and re-layouts: 6.87 us -> 0 us
    unnamed x4 -> x0, local copies, waits for them, and re-layouts: 6.87 us -> none
    pallas_call x0 -> x1, Pallas kernels: none -> 3.37 us  [body(): pl.pallas_call(write_out, out_shape=(pltpu.HBM(tracer.shape, tracer.dtype...]
    pallas_call x1, Pallas kernels: 45.8 us -> 42.5 us  [body(): pl.pallas_call(functools.partial(kernel, counts), out_shape=(block, block...]
where the time goes in v2:
time: 46.7 us; the launch traced here: 46.6 us
  Pallas kernels  45.9 us (98%)
  between operations  0.64 us (1%)
    pallas_call x1, Pallas kernels, body(): pl.pallas_call(functools.partial(kernel, counts), out_shape=(block, block...  42.5 us
    pallas_call x1, Pallas kernels, body(): pl.pallas_call(write_out, out_shape=(pltpu.HBM(tracer.shape, tracer.dtype...  3.37 us

profile of v2, /device:TPU:0, one launch (start us, length us, event | category | flops | bytes accessed | tf_op | source)
XLA Modules:
  0.0 46.6 jit_solution(8817147043713142505)
XLA Ops:
  0.6 42.5 %shard_map.50 = (f32[4,16,128,128]{3,2,1,0:T(8,128)S(1)}, f32[4,16,128,128]{3,2,1,0:T(8,128)S(1)}) custom-call(f32[4,16,128,128]{3,2,1,0:T(8,128)} %tracer.1, f32[4,16,128,128]{3,2,1,0:T(8,128)} %mobility.1, f32[4,16,128,128]{3,2,1,0:T(8,128)} %source.1), custom_call_target="tpu_custom_call" | custom-call | tf_op jit(solution)/shard_map/pallas_call | solution.py:260
  43.2 3.4 %shard_map.51 = (f32[4,16,128,128]{3,2,1,0:T(8,128)}, f32[4,16,128,128]{3,2,1,0:T(8,128)}) custom-call(f32[4,16,128,128]{3,2,1,0:T(8,128)S(1)} %get-tuple-element.4.standardized, f32[4,16,128,128]{3,2,1,0:T(8,128)S(1)} %get-tuple-element.5.end), custom_call_target="tpu_custom_call" | custom-call | tf_op jit(solution)/shard_map/pallas_call | solution.py:278

commit v3 on v2

--- a/solution.py
+++ b/solution.py
@@ -11,6 +11,7 @@
 PAD = 8
 ROWS = 32
 EPS = 0.0001
+HOLD = 1
 
 
 def kernel(
@@ -57,12 +58,14 @@
 
     def face(step, side):
         from_, to, offset = ((1, nx + 1, -1), (nx, 0, 1))[side]
-        return send(
-            fields[step],
-            (inner_y, pl.ds(from_, 1), line),
-            (inner_y, pl.ds(to, 1), line),
-            (x_send, x_recv), (step, side), peer("east", offset),
-        )
+        return [
+            send(
+                fields[step],
+                (inner_y, pl.ds(from_, 1), line),
+                (inner_y, pl.ds(to, 1), line),
+                (x_send, x_recv), (step, side), peer("east", offset),
+            )
+        ]
 
     def borders(step, group):
         columns = groups[group]
@@ -82,15 +85,14 @@
             ))
         return copies
 
-    def moments(group):
-        columns = groups[group]
+    def moments(columns, at):
         inside = pl.ds(columns.start - 1, columns.size)
         return [
             pltpu.make_async_remote_copy(
                 src_ref=stats.at[0, inside],
                 dst_ref=stats.at[j, inside],
-                send_sem=s_send.at[j - 1, group],
-                recv_sem=s_recv.at[j - 1, group],
+                send_sem=s_send.at[j - 1, at],
+                recv_sem=s_recv.at[j - 1, at],
                 device_id=peer("down", j),
                 device_id_type=MESH,
             )
@@ -113,7 +115,9 @@
 
     faces = [[face(step, side) for side in (0, 1)] for step in range(3)]
     edges = [[borders(step, group) for group in range(3)] for step in range(3)]
-    spread_moments = [moments(group) for group in range(3)]
+    middle_moments, low_moments, high_moments = [
+        moments(columns, at) for at, columns in enumerate(groups)
+    ]
 
     def column(step, x):
         field = fields[step]
@@ -139,16 +143,16 @@
             values = end[y, x - 1]
             mean = jnp.sum(values, axis=0, keepdims=True) * (1.0 / nz)
             off = values - mean
-            stats[0, x - 1, pl.ds(y, 1)] = mean
-            stats[0, x - 1, pl.ds(ny + y, 1)] = jnp.sum(off * off, axis=0, keepdims=True)
+            stats[0, x - 1, pl.ds(2 * y, 1)] = mean
+            stats[0, x - 1, pl.ds(2 * y + 1, 1)] = jnp.sum(off * off, axis=0, keepdims=True)
 
     def finish(x):
         for y in range(ny):
-            means = [stats[j, x - 1, pl.ds(y, 1)] for j in range(n_down)]
+            means = [stats[j, x - 1, pl.ds(2 * y, 1)] for j in range(n_down)]
             mean = sum(means[1:], means[0]) * (1.0 / n_down)
-            squares = stats[0, x - 1, pl.ds(ny + y, 1)]
+            squares = stats[0, x - 1, pl.ds(2 * y + 1, 1)]
             for j in range(1, n_down):
-                squares += stats[j, x - 1, pl.ds(ny + y, 1)]
+                squares += stats[j, x - 1, pl.ds(2 * y + 1, 1)]
             for value in means:
                 squares += nz * ((value - mean) * (value - mean))
             scale = lax.rsqrt(squares * (1.0 / (nz * n_down)) + EPS)
@@ -166,43 +170,56 @@
             copy.wait_recv()
 
     loads[0].wait()
-    start([faces[0][0]])
     loads[1].wait()
-    start([faces[0][1]])
+    ahead = lax.rem(me["south"], 2) == 0
+    both = faces[0][0] + faces[0][1]
+    started.extend(both)
+
+    @pl.when(ahead)
+    def _():
+        for copy in both:
+            copy.start()
+
     loads[2].wait()
-    for group in range(3):
+    for group in (1, 2, 0):
         start(edges[0][group])
+    received(edges[0][1][:HOLD])
+
+    @pl.when(jnp.logical_not(ahead))
+    def _():
+        for copy in both:
+            copy.start()
+
     loads[3].wait()
     loads[4].wait()
-    for group in range(3):
-        received(edges[0][group])
+    received(edges[0][1][HOLD:] + edges[0][2] + edges[0][0])
     over_middle(functools.partial(column, 0))
     start(edges[1][0])
 
-    received([faces[0][0]])
+    received(faces[0][0])
     column(0, nx)
-    start([faces[1][1]])
+    start(faces[1][1])
     start(edges[1][2])
 
-    received([faces[0][1]])
+    received(faces[0][1])
     column(0, 1)
-    start([faces[1][0]])
+    start(faces[1][0])
     start(edges[1][1])
 
     received(edges[1][0])
     over_middle(functools.partial(column, 1))
     start(edges[2][0])
 
-    received([faces[1][1]])
+    received(faces[1][1])
     received(edges[1][1])
     column(1, 1)
-    start([faces[2][0]])
+    start(faces[2][0])
     start(edges[2][1])
 
-    received([faces[1][0]])
+    received(faces[1][0])
     received(edges[1][2])
     column(1, nx)
-    start([faces[2][1]])
+    start(faces[2][1])
     start(edges[2][2])
 
     def last(x):
@@ -211,23 +228,21 @@
 
     received(edges[2][0])
     over_middle(last)
-    start(spread_moments[0])
-    received(spread_moments[0])
+    start(middle_moments)
+    received(middle_moments)
     over_middle(finish)
 
-    received([faces[2][0]])
+    def last_edge(x, arriving, travelling):
+        received(arriving)
+        last(x)
+        start(travelling)
+        received(travelling)
+        finish(x)
+
     received(edges[2][2])
-    last(nx)
-    start(spread_moments[2])
-    received(spread_moments[2])
-    finish(nx)
-
-    received([faces[2][1]])
+    last_edge(nx, faces[2][0], high_moments)
     received(edges[2][1])
-    last(1)
-    start(spread_moments[1])
-    received(spread_moments[1])
-    finish(1)
+    last_edge(1, faces[2][1], low_moments)
 
     for copy in started:
         copy.wait_send()

time: 46.7 us -> 46.1 us (0.987)
  Pallas kernels: 45.9 us -> 45.1 us
    pallas_call x1, Pallas kernels: 42.5 us -> 41.7 us  [body(): pl.pallas_call(functools.partial(kernel, counts), out_shape=(block, block...]
where the time goes in v3:
time: 46.1 us; the launch traced here: 45.7 us
  Pallas kernels  45.1 us (98%)
  between operations  0.64 us (1%)
    pallas_call x1, Pallas kernels, body(): pl.pallas_call(functools.partial(kernel, counts), out_shape=(block, block...  41.7 us
    pallas_call x1, Pallas kernels, body(): pl.pallas_call(write_out, out_shape=(pltpu.HBM(tracer.shape, tracer.dtype...  3.37 us

profile of v3, /device:TPU:0, one launch (start us, length us, event | category | flops | bytes accessed | tf_op | source)
XLA Modules:
  0.0 45.7 jit_solution(12226767333150346654)
XLA Ops:
  0.6 41.7 %shard_map.50 = (f32[4,16,128,128]{3,2,1,0:T(8,128)S(1)}, f32[4,16,128,128]{3,2,1,0:T(8,128)S(1)}) custom-call(f32[4,16,128,128]{3,2,1,0:T(8,128)} %tracer.1, f32[4,16,128,128]{3,2,1,0:T(8,128)} %mobility.1, f32[4,16,128,128]{3,2,1,0:T(8,128)} %source.1), custom_call_target="tpu_custom_call" | custom-call | tf_op jit(solution)/shard_map/pallas_call | solution.py:275
  42.4 3.4 %shard_map.51 = (f32[4,16,128,128]{3,2,1,0:T(8,128)}, f32[4,16,128,128]{3,2,1,0:T(8,128)}) custom-call(f32[4,16,128,128]{3,2,1,0:T(8,128)S(1)} %get-tuple-element.4.standardized, f32[4,16,128,128]{3,2,1,0:T(8,128)S(1)} %get-tuple-element.5.end), custom_call_target="tpu_custom_call" | custom-call | tf_op jit(solution)/shard_map/pallas_call | solution.py:293
